TPU v7x, 32 devices: a whole 2x2x4 slice. The times are simulated.
32 devices in a mesh: dp: 2 (over x), tp: 4 (over z), pp: 4 (over y, core).
Axes of the slice: x: 2, y: 2, z: 4, core: 2. Of those that a mesh axis runs over, the one named last changes fastest.
Arguments:
- hidden: bfloat16 [4, 64, 2048], P('dp'), parts along dimension 0
- positions: int32 [4, 64], P('dp'), parts along dimension 0
- key_cache: bfloat16 [4, 4, 64, 4, 512, 64], P('pp', 'dp', None, 'tp'), parts along dimension 1
- value_cache: bfloat16 [4, 4, 64, 4, 512, 64], P('pp', 'dp', None, 'tp'), parts along dimension 1
- attn_norm: bfloat16 [4, 2048], P('pp')
- w_query: bfloat16 [4, 2048, 2048], P('pp', None, 'tp')
- w_key: bfloat16 [4, 2048, 256], P('pp', None, 'tp')
- w_value: bfloat16 [4, 2048, 256], P('pp', None, 'tp')
- w_out: bfloat16 [4, 2048, 2048], P('pp', 'tp')
- mlp_norm: bfloat16 [4, 2048], P('pp')
- w_gate: bfloat16 [4, 2048, 5632], P('pp', None, 'tp')
- w_up: bfloat16 [4, 2048, 5632], P('pp', None, 'tp')
- w_down: bfloat16 [4, 5632, 2048], P('pp', 'tp')
Outputs:
- output 1: bfloat16 [4, 64, 2048], P('dp'), parts along dimension 0
- output 2: bfloat16 [4, 4, 64, 4, 512, 64], P('pp', 'dp', None, 'tp'), parts along dimension 1
- output 3: bfloat16 [4, 4, 64, 4, 512, 64], P('pp', 'dp', None, 'tp'), parts along dimension 1
There are 2 independent parts. A program takes and returns all parts, laid end to end along the dimension named above; an argument that names none is the same for every part.
All inputs are finite; a program needn't handle non-finite values.
Results may differ from a plain program's by a relative error of at most 0.02.
Values are sent between devices in bfloat16 or wider.
A program may use at most 1 GiB of HBM per device.

v0:
```python
import math
import jax
import jax.numpy as jnp
from jax import lax
from jax.sharding import PartitionSpec as P

ROPE_THETA = 500000.0
SCALE_FACTOR = 8.0
LOW_FACTOR = 1.0
HIGH_FACTOR = 4.0
ORIG_CONTEXT = 8192.0
NORM_EPS = 1e-5


def rope_freqs(head_dim):
    freq_index = jnp.arange(head_dim // 2, dtype=jnp.float32)
    base_freq = ROPE_THETA ** (-2.0 * freq_index / head_dim)
    wave_len = 2.0 * math.pi / base_freq
    smooth_t = (ORIG_CONTEXT / wave_len - LOW_FACTOR) / (HIGH_FACTOR - LOW_FACTOR)
    mixed_freq = (1.0 - smooth_t) * base_freq / SCALE_FACTOR + smooth_t * base_freq
    long_freq = jnp.where(wave_len > ORIG_CONTEXT / LOW_FACTOR, base_freq / SCALE_FACTOR, mixed_freq)
    return jnp.where(wave_len < ORIG_CONTEXT / HIGH_FACTOR, base_freq, long_freq)


def rms_norm(values, gain_vec):
    values_f = values.astype(jnp.float32)
    inv_rms = lax.rsqrt(jnp.mean(values_f * values_f, axis=-1, keepdims=True) + NORM_EPS)
    return (values_f * inv_rms * gain_vec.astype(jnp.float32)).astype(jnp.bfloat16)


def rotate(values_f, cosine, sine_t):
    half_dim = values_f.shape[-1] // 2
    first_half = values_f[..., :half_dim]
    second_half = values_f[..., half_dim:]
    return jnp.concatenate([first_half * cosine - second_half * sine_t, second_half * cosine + first_half * sine_t], axis=-1)


def attention_part(tokens, key_cache, value_cache, positions, params):
    gain_attn, w_query, w_key, w_value, w_out = params
    n_groups, n_batch, kv_local, seq_len, head_dim = key_cache.shape
    heads_local = w_query.shape[-1] // head_dim
    gqa_size = heads_local // kv_local
    angles = positions.astype(jnp.float32)[..., None] * rope_freqs(head_dim)
    cosine = jnp.cos(angles)
    sine_t = jnp.sin(angles)
    normed = rms_norm(tokens, gain_attn)
    query_f = jnp.einsum("mbd,dh->mbh", normed, w_query, preferred_element_type=jnp.float32)
    query_h = rotate(query_f.reshape(n_groups, n_batch, kv_local, gqa_size, head_dim), cosine[:, :, None, None, :], sine_t[:, :, None, None, :]).astype(jnp.bfloat16)
    key_f = jnp.einsum("mbd,dh->mbh", normed, w_key, preferred_element_type=jnp.float32)
    key_new = rotate(key_f.reshape(n_groups, n_batch, kv_local, head_dim), cosine[:, :, None, :], sine_t[:, :, None, :]).astype(jnp.bfloat16)
    value_new = jnp.einsum("mbd,dh->mbh", normed, w_value, preferred_element_type=jnp.float32).astype(jnp.bfloat16).reshape(n_groups, n_batch, kv_local, head_dim)
    seq_rows = jnp.arange(seq_len)
    row_hit = (seq_rows == positions[..., None])[:, :, None, :, None]
    key_cache = jnp.where(row_hit, key_new[:, :, :, None, :], key_cache)
    value_cache = jnp.where(row_hit, value_new[:, :, :, None, :], value_cache)
    scores = jnp.einsum("mbkgd,mbksd->mbkgs", query_h, key_cache, preferred_element_type=jnp.float32) * head_dim ** -0.5
    visible = (seq_rows <= positions[..., None])[:, :, None, None, :]
    attn_probs = jax.nn.softmax(jnp.where(visible, scores, -jnp.inf), axis=-1).astype(jnp.bfloat16)
    attn_vals = jnp.einsum("mbkgs,mbksd->mbkgd", attn_probs, value_cache, preferred_element_type=jnp.float32).astype(jnp.bfloat16).reshape(n_groups, n_batch, heads_local * head_dim)
    attn_partial = jnp.einsum("mbh,hd->mbd", attn_vals, w_out, preferred_element_type=jnp.float32).astype(jnp.bfloat16)
    return attn_partial, key_cache, value_cache


def mlp_part(mid_state, gain_mlp, w_gate, w_up, w_down):
    normed_mlp = rms_norm(mid_state, gain_mlp)
    gate_f = jnp.einsum("mbd,df->mbf", normed_mlp, w_gate, preferred_element_type=jnp.float32)
    up_f = jnp.einsum("mbd,df->mbf", normed_mlp, w_up, preferred_element_type=jnp.float32)
    act_bf = (jax.nn.silu(gate_f) * up_f).astype(jnp.bfloat16)
    return jnp.einsum("mbf,fd->mbd", act_bf, w_down, preferred_element_type=jnp.float32).astype(jnp.bfloat16)


def solution(mesh):
    n_stages = mesh.shape["pp"]
    cache_spec = P("pp", "dp", None, "tp", None, None)
    col_spec = P("pp", None, "tp")
    row_spec = P("pp", "tp", None)
    gain_spec = P("pp", None)
    in_specs = (P("dp", None, None), P("dp", None), cache_spec, cache_spec, gain_spec, col_spec, col_spec, col_spec, row_spec, gain_spec, col_spec, col_spec, row_spec)
    out_specs = (P("dp", None, None), cache_spec, cache_spec)

    def per_device(hidden, positions, key_cache, value_cache, attn_norm, w_query, w_key, w_value, w_out, mlp_norm, w_gate, w_up, w_down):
        stage_idx = lax.axis_index("pp")
        attn_params = (attn_norm[0], w_query[0], w_key[0], w_value[0], w_out[0])
        gain_mlp = mlp_norm[0]
        gate_w = w_gate[0]
        up_w = w_up[0]
        down_w = w_down[0]

        def attn_run(carry_in):
            state_in, key_in, value_in = carry_in
            return attention_part(state_in, key_in, value_in, positions, attn_params)

        def attn_skip(carry_in):
            state_in, key_in, value_in = carry_in
            return jnp.zeros_like(state_in), key_in, value_in

        def mlp_run(mid_in):
            return mlp_part(mid_in, gain_mlp, gate_w, up_w, down_w)

        def mlp_skip(mid_in):
            return jnp.zeros_like(mid_in)

        state_h = hidden
        key_local = key_cache[0]
        value_local = value_cache[0]
        for step_idx in range(n_stages):
            active = stage_idx == step_idx
            attn_partial, key_local, value_local = lax.cond(active, attn_run, attn_skip, (state_h, key_local, value_local))
            attn_out = lax.psum(attn_partial, "tp")
            mid_state = (state_h.astype(jnp.float32) + attn_out.astype(jnp.float32)).astype(jnp.bfloat16)
            mlp_out = lax.psum(lax.cond(active, mlp_run, mlp_skip, mid_state), "tp")
            state_h = (mid_state.astype(jnp.float32) + mlp_out.astype(jnp.float32)).astype(jnp.bfloat16)
            if step_idx + 1 < n_stages:
                state_h = lax.ppermute(state_h, "pp", [(step_idx, step_idx + 1)])
        final_state = lax.psum(state_h, "pp")
        return final_state, key_local[None], value_local[None]

    return jax.shard_map(per_device, mesh=mesh, in_specs=in_specs, out_specs=out_specs, check_vma=False)
```

profile of v0, /device:TPU:0, one launch (start us, length us, event | category | flops | bytes accessed | tf_op | source)
XLA Modules:
  0.0 571.2 jit_solution(14998018634169682006)
XLA Ops:
  7.2 7.9 %copy.63 = bf16[1,2,64,1,512,64]{4,5,3,2,1,0:T(8,128)(2,1)} copy(bf16[1,2,64,1,512,64]{4,5,3,2,1,0:T(8,128)(2,1)} %param.31) | data formatting | bytes 16777216
  15.1 8.0 %copy.64 = bf16[1,2,64,1,512,64]{4,5,3,2,1,0:T(8,128)(2,1)} copy(bf16[1,2,64,1,512,64]{4,5,3,2,1,0:T(8,128)(2,1)} %param.32) | data formatting | bytes 16777216
  23.3 31.2 %conditional.8 = (bf16[2,64,2048]{2,1,0:T(8,128)(2,1)}, bf16[2,64,1,512,64]{3,4,1,0,2:T(8,128)(2,1)}, bf16[2,64,1,512,64]{3,4,1,0,2:T(8,128)(2,1)}) conditional(s32[]{:T(128)} %convert_element_type.297, (bf16[2,64,1,512,64]{3,4,1,0,2:T(8,128)(2,1)}, bf16[2,64,1,512,64]{3,4,1,0,2:T(8,128)(2,1)}) %tuple.142, (s32[2,64]{1,0:T(2,128)S(1)}, ...), branch_computations={%region_0.0_spmd, %region_1.5_spmd} | conditional | flops 754732288 | bytes 64276376 | solution.py:108
  23.3 0.2 fusion.12
  23.5 0.4 convolution_bitcast_fusion
  24.0 0.2 fusion.38
  24.2 0.1 copy.16
  24.3 0.4 convolution_convert_fusion.1
  24.7 0.1 iota_compare_fusion.1
  24.9 12.0 %broadcast_select_fusion.1 = (bf16[2,64,1,512,64]{3,4,1,0,2:T(8,128)(2,1)}, bf16[2,64,1,512,64]{3,4,1,0,2:T(8,128)(2,1)}) fusion(bf16[2,64,1,512,64]{3,4,1,0,2:T(8,128)(2,1)} %get-tuple-element.147, pred[2,64,512]{2,1,0:T(8,128)(4,1)S(1)} %get-tuple-element.240, bf16[2,64,64]{2,1,0:T(8,128)(2,1)S(1)} %copy.16, ...), kind=kLoop, calls=%fused_computation.6 | loop fusion | flops 8388608 | bytes 33652736 | tf_op jit(solution)/shard_map/cond/branch_1_fun/jit(_where)/select_n | solution.py:54
  36.9 0.5 fusion.6
  37.4 0.1 reshape.586
  37.5 0.3 multiply_cosine_fusion
  37.8 0.9 fusion.22
  38.8 6.3 %fusion.268 = (f32[2,64,8]{2,1,0:T(8,128)S(1)}, f32[2,64,8,512]{3,2,1,0:T(8,128)}) fusion(pred[2,64,512]{2,1,0:T(8,128)(4,1)S(1)} %get-tuple-element.239, bf16[2,64,1,512,64]{3,4,1,0,2:T(8,128)(2,1)} %get-tuple-element.283, bf16[2,64,8,32]{3,2,1,0:T(8,128)(2,1)} %get-tuple-element.232, bf16[2,64,8,32]{3,2,1,0:T(8,128)(2,1)S(1)} %get-tuple-element.231), kind=kOutput, calls=%fused_computation.312 | convolution fusion | flops 69468672 | bytes 10686464 | tf_op jit(solution)/shard_map/cond/branch_1_fun/sub | solution.py:58
  45.1 6.3 %fusion.9 = bf16[2,64,8,64]{3,2,1,0:T(8,128)(2,1)S(1)} fusion(bf16[2,64,1,512,64]{3,4,1,0,2:T(8,128)(2,1)} %get-tuple-element.284, f32[2,64,8,512]{3,2,1,0:T(8,128)} %get-tuple-element.242, f32[2,64,8]{2,1,0:T(8,128)S(1)} %get-tuple-element.241), kind=kOutput, calls=%fused_computation.17 | convolution fusion | flops 68222976 | bytes 10620928 | tf_op jit(solution)/shard_map/cond/branch_1_fun/mbkgs,mbksd->mbkgd/dot_general | solution.py:59
  51.4 0.2 reshape.590
  51.7 2.8 convolution_convert_fusion
  54.5 0.0 all-reduce.12.cloned.1.call-start
  54.6 40.4 %all-reduce.10.cloned.1.call-done = bf16[2,64,2048]{2,1,0:T(8,128)(2,1)} async-done(((bf16[2,64,2048]{2,1,0:T(8,128)(2,1)}), bf16[2,64,2048]{2,1,0:T(8,128)(2,1)}) %all-reduce.10.cloned.1.call-update) | async-done | bytes 524304 | tf_op jit(solution)/shard_map/psum | solution.py:109
  95.1 1.2 add_convert_fusion.11
  96.2 11.2 %conditional.9 = (bf16[2,64,2048]{2,1,0:T(8,128)(2,1)S(1)}) conditional(s32[]{:T(128)} %convert_element_type.297, () %tuple.66, (bf16[2,64,2048]{2,1,0:T(8,128)(2,1)S(1)}, bf16[2048]{0:T(1024)(128)(2,1)S(1)}, bf16[2048,1408]{1,0:T(8,128)(2,1)}, bf16[2048,1408]{1,0:T(8,128)(2,1)}, bf16[1408,2048]{1,0:T(8,128)(2,1)}) %tuple.165), branch_computations={%region_6.7_spmd, %region_7.9_spmd} | conditional | flops 2218821632 | bytes 20871688 | solution.py:111
  96.3 0.2 fusion.57
  96.5 4.5 fusion.46
  101.0 6.5 %fusion.54 = bf16[2,64,2048]{2,1,0:T(8,128)(2,1)S(1)} fusion(bf16[1408,2048]{1,0:T(8,128)(2,1)} %get-tuple-element.155, bf16[2048,1408]{1,0:T(8,128)(2,1)} %get-tuple-element.154, f32[2,64,1408]{2,1,0:T(8,128)} %fusion.46, bf16[2,64,2048]{2,1,0:T(8,128)(2,1)S(1)} %get-tuple-element.151, f32[2048]{0:T(1024)S(1)} %convert_element_type.225, ...), kind=kOutput, calls=%fused_computation.67 | convolution fusion | flops 1478787072 | bytes 13312512 | tf_op jit(solution)/shard_map/cond/branch_1_fun/mbf,fd->mbd/dot_general | solution.py:69
  107.5 0.8 copy-done.3
  108.3 0.0 all-reduce.14.cloned.1.call-start
  108.3 37.5 %all-reduce.12.cloned.1.call-done = bf16[2,64,2048]{2,1,0:T(8,128)(2,1)} async-done(((bf16[2,64,2048]{2,1,0:T(8,128)(2,1)}), bf16[2,64,2048]{2,1,0:T(8,128)(2,1)}) %all-reduce.12.cloned.1.call-update) | async-done | bytes 524304 | tf_op jit(solution)/shard_map/psum | solution.py:111
  145.9 2.0 add_convert_fusion.10
  147.8 1.3 collective-permute-start
  149.2 1.5 collective-permute-done
  150.6 1.0 conditional.10
  150.6 0.8 broadcast.716
  151.7 0.0 all-reduce.16.cloned.1.call-start
  151.7 68.8 %all-reduce.14.cloned.1.call-done = bf16[2,64,2048]{2,1,0:T(8,128)(2,1)} async-done(((bf16[2,64,2048]{2,1,0:T(8,128)(2,1)}), bf16[2,64,2048]{2,1,0:T(8,128)(2,1)}) %all-reduce.14.cloned.1.call-update) | async-done | bytes 524304 | tf_op jit(solution)/shard_map/psum | solution.py:109
  220.5 1.2 add_convert_fusion.9
  221.7 0.1 conditional.11
  221.8 0.8 copy-done.4
  222.6 0.0 all-reduce.18.cloned.1.call-start
  222.7 47.0 %all-reduce.16.cloned.1.call-done = bf16[2,64,2048]{2,1,0:T(8,128)(2,1)} async-done(((bf16[2,64,2048]{2,1,0:T(8,128)(2,1)}), bf16[2,64,2048]{2,1,0:T(8,128)(2,1)}) %all-reduce.16.cloned.1.call-update) | async-done | bytes 524304 | tf_op jit(solution)/shard_map/psum | solution.py:111
  269.7 2.0 add_convert_fusion.8
  271.6 0.7 collective-permute-start.1
  272.4 1.0 conditional.12
  272.4 0.8 broadcast.731
  273.4 0.0 all-reduce.20.cloned.1.call-start
  273.5 79.5 %all-reduce.18.cloned.1.call-done = bf16[2,64,2048]{2,1,0:T(8,128)(2,1)} async-done(((bf16[2,64,2048]{2,1,0:T(8,128)(2,1)}), bf16[2,64,2048]{2,1,0:T(8,128)(2,1)}) %all-reduce.18.cloned.1.call-update) | async-done | bytes 524304 | tf_op jit(solution)/shard_map/psum | solution.py:109
  353.0 1.2 add_convert_fusion.7
  354.2 0.1 conditional.13
  354.3 0.8 copy-done.5
  355.1 0.0 all-reduce.22.cloned.1.call-start
  355.1 49.6 %all-reduce.20.cloned.1.call-done = bf16[2,64,2048]{2,1,0:T(8,128)(2,1)} async-done(((bf16[2,64,2048]{2,1,0:T(8,128)(2,1)}), bf16[2,64,2048]{2,1,0:T(8,128)(2,1)}) %all-reduce.20.cloned.1.call-update) | async-done | bytes 524304 | tf_op jit(solution)/shard_map/psum | solution.py:111
  404.7 1.2 add_convert_fusion.6
  405.9 0.7 collective-permute-start.2
  406.6 0.3 conditional.14
  406.9 0.8 copy-done.6
  407.8 69.6 %all-reduce.22.cloned.1.call-done = bf16[2,64,2048]{2,1,0:T(8,128)(2,1)} async-done(((bf16[2,64,2048]{2,1,0:T(8,128)(2,1)}), bf16[2,64,2048]{2,1,0:T(8,128)(2,1)}) %all-reduce.22.cloned.1.call-update) | async-done | bytes 524304 | tf_op jit(solution)/shard_map/psum | solution.py:109
  477.4 1.2 add_convert_fusion.5
  478.6 0.1 conditional.15
  478.7 0.8 copy-done.7
  479.5 0.0 all-reduce.26.cloned.1.call-start
  479.5 46.9 %all-reduce.24.cloned.1.call-done = bf16[2,64,2048]{2,1,0:T(8,128)(2,1)} async-done(((bf16[2,64,2048]{2,1,0:T(8,128)(2,1)}), bf16[2,64,2048]{2,1,0:T(8,128)(2,1)}) %all-reduce.24.cloned.1.call-update) | async-done | bytes 524304 | tf_op jit(solution)/shard_map/psum | solution.py:111
  526.4 2.0 add_convert_fusion.4
  528.4 34.0 %all-reduce.26.cloned.1.call-done = bf16[2,64,2048]{2,1,0:T(8,128)(2,1)} async-done(((bf16[2,64,2048]{2,1,0:T(8,128)(2,1)}), bf16[2,64,2048]{2,1,0:T(8,128)(2,1)}) %all-reduce.26.cloned.1.call-update) | async-done | bytes 524304 | tf_op jit(solution)/shard_map/psum | solution.py:115
  562.4 1.9 copy.65
  (51 shorter events, 0.6 us)
Async XLA Ops:
  7.2 87.9 %all-reduce.10.cloned.1.call-start = ((), (), s32[]{:S(2)}) async-start(), calls=%async_computation | async-start | bytes 1048576 | tf_op jit(solution)/shard_map/psum | solution.py:109
  15.1 8.1 %copy-start.9 = (bf16[1,2048]{1,0:T(2,128)(2,1)S(1)}, bf16[1,2048]{1,0:T(2,128)(2,1)}, u32[]{:S(2)}) copy-start(bf16[1,2048]{1,0:T(2,128)(2,1)} %param.33) | copy-start | bytes 12292
  15.1 8.1 %copy-start = (bf16[1,2048,512]{2,1,0:T(8,128)(2,1)S(1)}, bf16[1,2048,512]{2,1,0:T(8,128)(2,1)}, u32[]{:S(2)}) copy-start(bf16[1,2048,512]{2,1,0:T(8,128)(2,1)} %param.34) | copy-start | bytes 6291460
  15.1 8.1 %copy-start.2 = (bf16[2,64,2048]{2,1,0:T(8,128)(2,1)S(1)}, bf16[2,64,2048]{2,1,0:T(8,128)(2,1)}, u32[]{:S(2)}) copy-start(bf16[2,64,2048]{2,1,0:T(8,128)(2,1)} %param.29) | copy-start | bytes 1572868
  15.1 8.1 %copy-start.8 = (s32[2,64]{1,0:T(2,128)S(1)}, s32[2,64]{1,0:T(2,128)}, u32[]{:S(2)}) copy-start(s32[2,64]{1,0:T(2,128)} %param.30) | copy-start | bytes 1540
  15.1 8.1 %copy-start.11 = (bf16[1,2048,64]{1,2,0:T(8,128)(2,1)S(1)}, bf16[1,2048,64]{1,2,0:T(8,128)(2,1)}, u32[]{:S(2)}) copy-start(bf16[1,2048,64]{1,2,0:T(8,128)(2,1)} %param.35) | copy-start | bytes 786436
  15.1 8.1 %copy-start.15 = (bf16[1,2048,64]{1,2,0:T(8,128)(2,1)S(1)}, bf16[1,2048,64]{1,2,0:T(8,128)(2,1)}, u32[]{:S(2)}) copy-start(bf16[1,2048,64]{1,2,0:T(8,128)(2,1)} %param.36) | copy-start | bytes 786436
  23.3 31.3 %copy-start.10 = (bf16[1,2048]{1,0:T(2,128)(2,1)S(1)}, bf16[1,2048]{1,0:T(2,128)(2,1)}, u32[]{:S(2)}) copy-start(bf16[1,2048]{1,0:T(2,128)(2,1)} %param.38) | copy-start | bytes 12292
  54.5 91.4 %all-reduce.12.cloned.1.call-start = ((), (), s32[]{:S(2)}) async-start(), calls=%async_computation.1 | async-start | bytes 1048576 | tf_op jit(solution)/shard_map/psum | solution.py:111
  96.2 54.4 %copy-start.12 = (bf16[1,2048,64]{1,2,0:T(8,128)(2,1)S(1)}, bf16[1,2048,64]{1,2,0:T(8,128)(2,1)}, u32[]{:S(2)}) copy-start(bf16[1,2048,64]{1,2,0:T(8,128)(2,1)} %param.35) | copy-start | bytes 786436
  107.5 0.8 copy-start.3
  108.3 112.2 %all-reduce.14.cloned.1.call-start = ((), (), s32[]{:S(2)}) async-start(), calls=%async_computation.2 | async-start | bytes 1048576 | tf_op jit(solution)/shard_map/psum | solution.py:109
  147.8 2.8 collective-permute-start
  151.7 118.0 %all-reduce.16.cloned.1.call-start = ((), (), s32[]{:S(2)}) async-start(), calls=%async_computation.3 | async-start | bytes 1048576 | tf_op jit(solution)/shard_map/psum | solution.py:111
  221.7 50.6 %copy-start.13 = (bf16[1,2048,64]{1,2,0:T(8,128)(2,1)S(1)}, bf16[1,2048,64]{1,2,0:T(8,128)(2,1)}, u32[]{:S(2)}) copy-start(bf16[1,2048,64]{1,2,0:T(8,128)(2,1)} %param.35) | copy-start | bytes 786436
  221.8 0.8 copy-start.4
  222.6 130.4 %all-reduce.18.cloned.1.call-start = ((), (), s32[]{:S(2)}) async-start(), calls=%async_computation.4 | async-start | bytes 1048576 | tf_op jit(solution)/shard_map/psum | solution.py:109
  271.6 0.7 collective-permute-start.1
  273.4 131.3 %all-reduce.20.cloned.1.call-start = ((), (), s32[]{:S(2)}) async-start(), calls=%async_computation.5 | async-start | bytes 1048576 | tf_op jit(solution)/shard_map/psum | solution.py:111
  354.2 52.4 %copy-start.14 = (bf16[1,2048,64]{1,2,0:T(8,128)(2,1)S(1)}, bf16[1,2048,64]{1,2,0:T(8,128)(2,1)}, u32[]{:S(2)}) copy-start(bf16[1,2048,64]{1,2,0:T(8,128)(2,1)} %param.35) | copy-start | bytes 786436
  354.3 0.8 copy-start.5
  355.1 122.3 %all-reduce.22.cloned.1.call-start = ((), (), s32[]{:S(2)}) async-start(), calls=%async_computation.6 | async-start | bytes 1048576 | tf_op jit(solution)/shard_map/psum | solution.py:109
  405.9 0.7 collective-permute-start.2
  406.9 0.8 copy-start.6
  407.7 118.6 %all-reduce.24.cloned.1.call-start = ((), (), s32[]{:S(2)}) async-start(), calls=%async_computation.7 | async-start | bytes 1048576 | tf_op jit(solution)/shard_map/psum | solution.py:111
  478.7 0.8 copy-start.7
  479.5 82.9 %all-reduce.26.cloned.1.call-start = ((), (), s32[]{:S(2)}) async-start(), calls=%async_computation.8 | async-start | bytes 1048576 | tf_op jit(solution)/shard_map/psum | solution.py:115
Sparse Core Ops, SparseCore 0:
  54.6 40.3 all-reduce.9
  108.4 37.4 all-reduce.11
  151.8 68.7 all-reduce.13
  223.3 46.3 all-reduce.15
  273.6 79.3 all-reduce.17
  355.8 48.8 all-reduce.19
  407.9 69.5 all-reduce.21
  480.3 46.0 all-reduce.23
  529.3 32.9 all-reduce.25
where the time goes:
time: 580 us; the launch traced here: 571 us
  waiting for transfers between devices  475 us (82%)
  matrix products  27.8 us (5%)
  other arithmetic  25.8 us (4%)
  local copies, waits for them, and re-layouts  24.1 us (4%)
  between operations  14.6 us (3%)
    psum x4, waiting for transfers between devices, per_device(): attn_out = lax.psum(attn_partial, 'tp')  258 us
    psum x4, waiting for transfers between devices, per_device(): mlp_out = lax.psum(lax.cond(active, mlp_run, mlp_skip, mid_state), 'tp')  181 us
    psum x1, waiting for transfers between devices, per_device(): final_state = lax.psum(state_h, 'pp')  34 us
    unnamed x33, local copies, waits for them, and re-layouts  21.8 us
    select_n x1, other arithmetic, attention_part(): key_cache = jnp.where(row_hit, key_new[:, :, :, None, :], key_cache)  12 us
  transfers between devices with their start and end apart: 12, of which 10 were waited for; matrix products, arithmetic and copies ran while one was open for 0% of the time, Pallas kernels for 0%

commit v1 on v0

v1 whole, which is shorter than its diff:
```python
import functools
import math
import jax
import jax.numpy as jnp
from jax import lax
from jax.experimental import pallas as pl
from jax.experimental.pallas import tpu as pltpu
from jax.sharding import PartitionSpec as P

ROPE_THETA = 500000.0
SCALE_FACTOR = 8.0
LOW_FACTOR = 1.0
HIGH_FACTOR = 4.0
ORIG_CONTEXT = 8192.0
NORM_EPS = 1e-5

MESH = pl.DeviceIdType.MESH
F32 = jnp.float32
BF16 = jnp.bfloat16

T = 64
NC = 4


def rope_freqs(head_dim):
    freq_index = jnp.arange(head_dim // 2, dtype=F32)
    base_freq = ROPE_THETA ** (-2.0 * freq_index / head_dim)
    wave_len = 2.0 * math.pi / base_freq
    smooth_t = (ORIG_CONTEXT / wave_len - LOW_FACTOR) / (HIGH_FACTOR - LOW_FACTOR)
    mixed_freq = (1.0 - smooth_t) * base_freq / SCALE_FACTOR + smooth_t * base_freq
    long_freq = jnp.where(wave_len > ORIG_CONTEXT / LOW_FACTOR, base_freq / SCALE_FACTOR, mixed_freq)
    return jnp.where(wave_len < ORIG_CONTEXT / HIGH_FACTOR, base_freq, long_freq)


def dot(lhs, rhs):
    return jnp.dot(lhs, rhs, preferred_element_type=F32)


def dot_nt(lhs, rhs):
    return lax.dot_general(lhs, rhs, (((1,), (1,)), ((), ())), preferred_element_type=F32)


def layer_kernel(
    nm, hid_hbm, pos_ref, cos_ref, sin_ref, ga_ref, gm_ref, wq_hbm, wk_hbm, wv_hbm, wo_hbm, wg_hbm, wu_hbm, wd_hbm, kc_hbm, vc_hbm,
    out_ref, kv_ref,
    wq, wkv, wo, wgu, wd, kc, vc, hin, hmid, norm, qs, ks, vs, att, act, part, send_a, recv_a, recv_b, nxt, fin,
    w_sem, kv_sem, h_sem, hin_sem, hmid_sem, a_sem, b_sem, fin_sem, sa_sem, sm_sem, sn_sem, sf_sem,
):
    tp = lax.axis_index("tp")
    pp = lax.axis_index("pp")
    n_tp, n_pp = 4, 4
    last = n_pp - 1
    is_end = (tp == 0) | (tp == n_tp - 1)
    is_mid = jnp.logical_not(is_end)
    side = tp + 1 - 2 * lax.rem(tp, 2)
    across = n_tp - 1 - tp
    d_model = norm.shape[-1]
    width = d_model // NC
    ff = act.shape[-1]

    def hidden_copy(i, c):
        return pltpu.make_async_copy(hid_hbm.at[i, :, pl.ds(c * width, width)], hin.at[i, c], h_sem.at[i, c])

    @pl.when(pp == 0)
    def _():
        for c in range(NC):
            hidden_copy(0, c).start()

    load_q = [pltpu.make_async_copy(wq_hbm, wq, w_sem.at[0])]
    load_kv = [
        pltpu.make_async_copy(wk_hbm, wkv.at[pl.ds(0, 64)], w_sem.at[1]),
        pltpu.make_async_copy(wv_hbm, wkv.at[pl.ds(64, 64)], w_sem.at[2]),
    ]
    load_o = [pltpu.make_async_copy(wo_hbm, wo, w_sem.at[3])]
    load_d = [pltpu.make_async_copy(wd_hbm, wd, w_sem.at[4])]
    load_gu = []
    for j in range(ff // 128):
        load_gu.append(pltpu.make_async_copy(wg_hbm.at[:, pl.ds(128 * j, 128)], wgu.at[:, pl.ds(256 * j, 128)], w_sem.at[5 + 2 * j]))
        load_gu.append(pltpu.make_async_copy(wu_hbm.at[:, pl.ds(128 * j, 128)], wgu.at[:, pl.ds(256 * j + 128, 128)], w_sem.at[6 + 2 * j]))

    def cache_copies(i):
        return [pltpu.make_async_copy(kc_hbm.at[i], kc.at[i], kv_sem.at[0, i]), pltpu.make_async_copy(vc_hbm.at[i], vc.at[i], kv_sem.at[1, i])]

    for copy in load_q + load_kv + cache_copies(0) + load_o + load_gu + load_d:
        copy.start()
    for i in range(1, nm):
        @pl.when(pp == 0)
        def _():
            for c in range(NC):
                hidden_copy(i, c).start()
        for copy in cache_copies(i):
            copy.start()

    barrier = pltpu.get_barrier_semaphore()
    me = tp * n_pp + pp
    for step in range(1, n_tp * n_pp):
        peer = lax.rem(me + step, n_tp * n_pp)
        pl.semaphore_signal(barrier, inc=1, device_id={"tp": peer // n_pp, "pp": lax.rem(peer, n_pp)}, device_id_type=MESH)
    pl.semaphore_wait(barrier, n_tp * n_pp - 1)

    def send(src, dst, s_sem, r_sem, to_tp, to_pp):
        return pltpu.make_async_remote_copy(src_ref=src, dst_ref=dst, send_sem=s_sem, recv_sem=r_sem, device_id={"tp": to_tp, "pp": to_pp}, device_id_type=MESH)

    def end_to_mid(i, k, c):
        return send(send_a.at[i, k, c], recv_a.at[i, k, c], sa_sem.at[i, k, c], a_sem.at[i, k, c], side, pp)

    def mid_to_mid(i, k, c):
        return send(send_a.at[i, k, c], recv_b.at[i, k, c], sa_sem.at[i, k, c], b_sem.at[i, k, c], across, pp)

    def mid_to_end(i, c):
        return send(hmid.at[i, c], hmid.at[i, c], sm_sem.at[i, c], hmid_sem.at[i, c], side, pp)

    def to_next(i, c):
        following = lax.rem(pp + 1, n_pp)
        return [
            send(nxt.at[i, c], hin.at[i, c], sn_sem.at[i, c, 0], hin_sem.at[i, c], tp, following),
            send(nxt.at[i, c], hin.at[i, c], sn_sem.at[i, c, 1], hin_sem.at[i, c], side, following),
        ]

    def fin_copy(i, c, slot, to_tp, to_pp):
        return send(fin.at[i, c], fin.at[i, c], sf_sem.at[i, c, slot], fin_sem.at[i, c], to_tp, to_pp)

    lane = lax.broadcasted_iota(jnp.int32, (8, 128), 1)
    row = lax.broadcasted_iota(jnp.int32, (8, 128), 0)
    upper = lane >= 64
    owner = [row == 2 * c + jnp.where(upper, 1, 0) for c in range(4)]
    lane_t = lax.broadcasted_iota(jnp.int32, (T, 128), 1)
    first_half = lax.rem(lane_t, 64) < 32
    lower_t = lane_t < 64
    lane_s = lax.broadcasted_iota(jnp.int32, (8, kc.shape[-1]), 1)

    def rms(src, i, gain_ref):
        total = jnp.zeros((T, 1), F32)
        for c in range(NC):
            x = src[i, c].astype(F32)
            total = total + jnp.sum(x * x, axis=-1, keepdims=True)
        inv = lax.rsqrt(total / d_model + NORM_EPS)
        for c in range(NC):
            cols = pl.ds(c * width, width)
            norm[:, cols] = (src[i, c].astype(F32) * inv * gain_ref[:, cols].astype(F32)).astype(BF16)

    def rotate(x, i):
        swapped = jnp.where(first_half, pltpu.roll(x, 96, 1), pltpu.roll(x, 32, 1))
        return x * cos_ref[i] + swapped * sin_ref[i]

    def attention_block(i, j):
        rows = pl.ds(pl.multiple_of(8 * j, 8), 8)
        cache_rows = pl.ds(pl.multiple_of(512 * j, 512), 512)
        kb = ks[rows, :]
        vb = vs[rows, :]
        seen = lane_s < pos_ref[i, rows, 0:1]
        lhs, fresh = [], []
        for h in range(8):
            x = qs[rows, pl.ds(128 * (h // 2), 128)]
            turned = pltpu.roll(x, 64, 1)
            both = jnp.where(upper, turned, x) if h % 2 == 0 else jnp.where(upper, x, turned)
            lhs.append(jnp.concatenate([jnp.where(o, both, 0.0) for o in owner], axis=1))
            fresh.append(jnp.sum(both * kb, axis=-1, keepdims=True) * 0.5)
        scores = dot(jnp.concatenate(lhs, axis=0).astype(BF16), kc[i, cache_rows, :])
        probs, new_probs = [], []
        for h in range(8):
            s = jnp.where(seen, scores[8 * h:8 * h + 8], -jnp.inf)
            top = jnp.maximum(jnp.max(s, axis=-1, keepdims=True), fresh[h])
            e = jnp.exp((s - top) * 0.125)
            e_new = jnp.exp((fresh[h] - top) * 0.125)
            scale = 1.0 / (jnp.sum(e, axis=-1, keepdims=True) + e_new)
            probs.append(e * scale)
            new_probs.append((e_new * scale).astype(BF16).astype(F32))
        mixed = dot_nt(jnp.concatenate(probs, axis=0).astype(BF16), vc[i, cache_rows, :])
        heads = []
        for h in range(8):
            o = mixed[8 * h:8 * h + 8]
            acc = jnp.where(owner[0], o[:, 0:128], 0.0)
            for c in range(1, 4):
                acc = acc + jnp.where(owner[c], o[:, 128 * c:128 * c + 128], 0.0)
            heads.append(acc + pltpu.roll(acc, 64, 1) + new_probs[h] * vb)
        for p in range(4):
            att[rows, pl.ds(128 * p, 128)] = jnp.where(upper, heads[2 * p + 1], heads[2 * p])

    def give_part(i, k, c, value):
        @pl.when(is_end)
        def _():
            send_a[i, k, c] = value.astype(BF16)
            end_to_mid(i, k, c).start()

        @pl.when(is_mid)
        def _():
            part[i, c] = value

    def attention(i, first):
        @pl.when(pp == 0)
        def _():
            for c in range(NC):
                hidden_copy(i, c).wait()

        @pl.when(pp > 0)
        def _():
            for c in range(NC):
                to_next(i, c)[0].wait_recv()

        rms(hin, i, ga_ref)

        @pl.when(first)
        def _():
            for copy in load_q + load_kv:
                copy.wait()

        n = norm[...]
        q = dot(n, wq[...])
        for p in range(4):
            qs[:, pl.ds(128 * p, 128)] = rotate(q[:, 128 * p:128 * p + 128], i).astype(BF16).astype(F32)
        kv = dot_nt(n, wkv[...])
        kv = jnp.where(lower_t, rotate(kv, i), kv).astype(BF16)
        kv_ref[i] = kv
        kv = kv.astype(F32)
        turned = pltpu.roll(kv, 64, 1)
        ks[...] = jnp.where(lower_t, kv, turned)
        vs[...] = jnp.where(lower_t, turned, kv)
        for copy in cache_copies(i):
            copy.wait()

        @pl.loop(0, T // 8)
        def _(j):
            attention_block(i, j)

        @pl.when(first)
        def _():
            for copy in load_o:
                copy.wait()

        a = att[...].astype(BF16)
        for c in range(NC):
            give_part(i, 0, c, dot(a, wo[:, pl.ds(c * width, width)]))

    def mid_sum(i, k):
        @pl.when(is_mid)
        def _():
            for c in range(NC):
                end_to_mid(i, k, c).wait_recv()
                send_a[i, k, c] = (part[i, c] + recv_a[i, k, c].astype(F32)).astype(BF16)
                mid_to_mid(i, k, c).start()

    def total_of(i, k, c):
        mid_to_mid(i, k, c).wait_recv()
        return (send_a[i, k, c].astype(F32) + recv_b[i, k, c].astype(F32)).astype(BF16).astype(F32)

    def attention_sum(i):
        @pl.when(is_mid)
        def _():
            for c in range(NC):
                hmid[i, c] = (hin[i, c].astype(F32) + total_of(i, 0, c)).astype(BF16)
                mid_to_end(i, c).start()

        @pl.when(is_end)
        def _():
            for c in range(NC):
                mid_to_end(i, c).wait_recv()

    def mlp(i, first):
        rms(hmid, i, gm_ref)

        @pl.when(first)
        def _():
            for copy in load_gu:
                copy.wait()

        n = norm[...]
        for j in range(ff // 128):
            both = dot(n, wgu[:, pl.ds(256 * j, 256)])
            gate = both[:, :128]
            act[:, pl.ds(128 * j, 128)] = (gate * jax.nn.sigmoid(gate) * both[:, 128:]).astype(BF16)

        @pl.when(first)
        def _():
            for copy in load_d:
                copy.wait()

        u = act[...]
        for c in range(NC):
            give_part(i, 1, c, dot(u, wd[:, pl.ds(c * width, width)]))

    def mlp_sum(i):
        @pl.when(is_mid & (pp < last))
        def _():
            for c in range(NC):
                nxt[i, c] = (hmid[i, c].astype(F32) + total_of(i, 1, c)).astype(BF16)
                for copy in to_next(i, c):
                    copy.start()

        @pl.when(is_mid & (pp == last))
        def _():
            for c in range(NC):
                fin[i, c] = (hmid[i, c].astype(F32) + total_of(i, 1, c)).astype(BF16)
                fin_copy(i, c, 0, side, last).start()
                fin_copy(i, c, 1, tp, last - 2).start()
                fin_copy(i, c, 2, tp, last - 1).start()

        @pl.when(is_end & (pp == last))
        def _():
            for c in range(NC):
                fin_copy(i, c, 0, side, last).wait_recv()
                fin_copy(i, c, 1, tp, last - 2).start()
                fin_copy(i, c, 2, tp, last - 1).start()

    @pl.loop(0, nm)
    def _(i):
        first = i == 0
        attention(i, first)
        mid_sum(i, 0)
        attention_sum(i)
        mlp(i, first)
        mid_sum(i, 1)
        mlp_sum(i)

    @pl.loop(0, nm)
    def _(i):
        @pl.when(pp < last)
        def _():
            for c in range(NC):
                fin_copy(i, c, 0, side, last).wait_recv()

                @pl.when(pp == last - 2)
                def _():
                    fin_copy(i, c, 0, tp, 0).start()

        for c in range(NC):
            out_ref[i, :, pl.ds(c * width, width)] = fin[i, c]

    @pl.loop(0, nm)
    def _(i):
        for c in range(NC):
            for k in range(2):
                end_to_mid(i, k, c).wait_send()

            @pl.when(is_mid)
            def _():
                mid_to_end(i, c).wait_send()

            @pl.when(is_mid & (pp < last))
            def _():
                for copy in to_next(i, c):
                    copy.wait_send()

            @pl.when((is_mid & (pp == last)) | (pp == last - 2))
            def _():
                fin_copy(i, c, 0, side, last).wait_send()

            @pl.when(pp == last)
            def _():
                fin_copy(i, c, 1, side, last).wait_send()
                fin_copy(i, c, 2, side, last).wait_send()


def run_layers(hidden, positions, key_cache, value_cache, attn_norm, w_query, w_key, w_value, w_out, mlp_norm, w_gate, w_up, w_down):
    n_groups, n_batch, d_model = hidden.shape
    seq, head = key_cache.shape[-2:]
    nm = n_groups * n_batch // T
    ff = w_gate.shape[-1]
    width = d_model // NC
    angles = positions.astype(F32)[..., None] * rope_freqs(head)
    cosine, sine = jnp.cos(angles), jnp.sin(angles)
    cos_t = jnp.concatenate([cosine] * 4, axis=-1).reshape(nm, T, 128)
    sin_t = jnp.concatenate([-sine, sine, -sine, sine], axis=-1).reshape(nm, T, 128)
    pos_t = jnp.broadcast_to(positions.reshape(nm, T, 1), (nm, T, 128))
    flat = lambda cache: jnp.swapaxes(cache, -1, -2).reshape(nm, T * head, seq)
    any_spec = pl.BlockSpec(memory_space=pl.ANY)
    vmem_spec = pl.BlockSpec(memory_space=pltpu.VMEM)
    dma = pltpu.SemaphoreType.DMA
    scratch = [
        pltpu.VMEM((d_model, 512), BF16),
        pltpu.VMEM((128, d_model), BF16),
        pltpu.VMEM((512, d_model), BF16),
        pltpu.VMEM((d_model, 2 * ff), BF16),
        pltpu.VMEM((ff, d_model), BF16),
        pltpu.VMEM((nm, T * head, seq), BF16),
        pltpu.VMEM((nm, T * head, seq), BF16),
        pltpu.VMEM((nm, NC, T, width), BF16),
        pltpu.VMEM((nm, NC, T, width), BF16),
        pltpu.VMEM((T, d_model), BF16),
        pltpu.VMEM((T, 512), F32),
        pltpu.VMEM((T, 128), F32),
        pltpu.VMEM((T, 128), F32),
        pltpu.VMEM((T, 512), F32),
        pltpu.VMEM((T, ff), BF16),
        pltpu.VMEM((nm, NC, T, width), F32),
        pltpu.VMEM((nm, 2, NC, T, width), BF16),
        pltpu.VMEM((nm, 2, NC, T, width), BF16),
        pltpu.VMEM((nm, 2, NC, T, width), BF16),
        pltpu.VMEM((nm, NC, T, width), BF16),
        pltpu.VMEM((nm, NC, T, width), BF16),
        dma((5 + 2 * (ff // 128),)),
        dma((2, nm)),
        dma((nm, NC)),
        dma((nm, NC)),
        dma((nm, NC)),
        dma((nm, 2, NC)),
        dma((nm, 2, NC)),
        dma((nm, NC)),
        dma((nm, 2, NC)),
        dma((nm, NC)),
        dma((nm, NC, 2)),
        dma((nm, NC, 3)),
    ]
    out, kv = pl.pallas_call(
        functools.partial(layer_kernel, nm),
        out_shape=(jax.ShapeDtypeStruct((nm, T, d_model), BF16), jax.ShapeDtypeStruct((nm, T, 2 * head), BF16)),
        in_specs=[any_spec] + [vmem_spec] * 5 + [any_spec] * 9,
        out_specs=(vmem_spec, vmem_spec),
        scratch_shapes=scratch,
        compiler_params=pltpu.CompilerParams(collective_id=0, has_side_effects=True, vmem_limit_bytes=64000000),
        name="layers",
    )(
        hidden.reshape(nm, T, d_model), pos_t, cos_t, sin_t, attn_norm, mlp_norm,
        w_query[0], jnp.swapaxes(w_key[0], 0, 1), jnp.swapaxes(w_value[0], 0, 1), w_out[0], w_gate[0], w_up[0], w_down[0],
        flat(key_cache[0]), flat(value_cache[0]),
    )
    kv = kv.reshape(n_groups, n_batch, 2 * head)
    row_hit = (jnp.arange(seq) == positions[..., None])[None, :, :, None, :, None]
    key_out = jnp.where(row_hit, kv[None, :, :, None, None, :head], key_cache)
    value_out = jnp.where(row_hit, kv[None, :, :, None, None, head:], value_cache)
    return out.reshape(n_groups, n_batch, d_model), key_out, value_out


def solution(mesh):
    cache_spec = P("pp", "dp", None, "tp", None, None)
    col_spec = P("pp", None, "tp")
    row_spec = P("pp", "tp", None)
    gain_spec = P("pp", None)
    in_specs = (P("dp", None, None), P("dp", None), cache_spec, cache_spec, gain_spec, col_spec, col_spec, col_spec, row_spec, gain_spec, col_spec, col_spec, row_spec)
    out_specs = (P("dp", None, None), cache_spec, cache_spec)
    return jax.shard_map(run_layers, mesh=mesh, in_specs=in_specs, out_specs=out_specs, check_vma=False)
```

time: 580 us -> 193 us (0.33); the launches traced: 571 us -> 193 us
  waiting for transfers between devices: 475 us -> 0 us
  Pallas kernels: 0 us -> 174 us
  matrix products: 27.8 us -> 0 us
  local copies, waits for them, and re-layouts: 24.1 us -> 3.1 us
  between operations: 14.6 us -> 0.67 us
  other arithmetic: 25.8 us -> 14.7 us
    psum x9 -> x0, waiting for transfers between devices: 473 us -> none  [the longest x4 258 us: per_device(): attn_out = lax.psum(attn_partial, 'tp')]
    pallas_call x0 -> x1, Pallas kernels: none -> 174 us  [run_layers(): pl.pallas_call(functools.partial(layer_kernel, nm), out_shape=(jax.ShapeD...]
    dot_general x7 -> x0, matrix products: 21.5 us -> none  [the longest x1 6.46 us: mlp_part(): jnp.einsum('mbf,fd->mbd', act_bf, w_down, preferred_element_type=jnp.floa...]
    unnamed x33 -> x3, local copies, waits for them, and re-layouts: 21.8 us -> 0.8 us
    convert_element_type x11 -> x1, other arithmetic: 11.7 us -> 0.69 us  [run_layers(): angles = positions.astype(F32)[..., None] * rope_freqs(head)]
    sub x1 -> x0, matrix products: 6.34 us -> none  [attention_part(): jax.nn.softmax(jnp.where(visible, scores, -jnp.inf), axis=-1)]
  transfers between devices with their start and end apart: 12 -> 0, of which waited for: 10 -> 0; matrix products, arithmetic and copies ran while one was open for 0% -> 0% of each run, Pallas kernels for 0% -> 0%
where the time goes in v1:
time: 193 us
  Pallas kernels  174 us (90%)
  other arithmetic  14.7 us (8%)
  local copies, waits for them, and re-layouts  3.1 us (2%)
    pallas_call x1, Pallas kernels, run_layers(): pl.pallas_call(functools.partial(layer_kernel, nm), out_shape=(jax.ShapeD...  174 us
    select_n x1, other arithmetic, run_layers(): jnp.where(row_hit, kv[None, :, :, None, None, head:], value_cache)  12.1 us

profile of v1, /device:TPU:0, one launch (start us, length us, event | category | flops | bytes accessed | tf_op | source)
XLA Modules:
  0.0 192.9 jit_solution(14237643123199243011)
XLA Ops:
  0.7 0.7 convert_element_type.3
  1.3 1.4 broadcast_in_dim.36.pos_ref
  2.7 0.8 iota_compare_fusion
  3.5 0.3 fusion
  3.8 0.8 pad_maximum_fusion
  4.7 174.4 %layers.1 = (bf16[2,64,2048]{2,1,0:T(8,128)(2,1)}, bf16[2,64,128]{2,1,0:T(8,128)(2,1)}) custom-call(bf16[2,64,2048]{2,1,0:T(8,128)(2,1)} %hid_hbm.1, s32[2,64,128]{2,1,0:T(8,128)} %broadcast_in_dim.36.pos_ref, f32[2,64,128]{2,1,0:T(8,128)} %get-tuple-element.14.cos_ref, f32[2,64,128]{2,1,0:T(8,128)} %get-tuple-element.15.sin_ref, bf16[1,2048]{1,0:T(2,128)(2,1)} %ga_ref.1, ...), custom_call_target="tpu_custom_call" | custom-call | tf_op jit(solution)/shard_map/layers/pallas_call | solution.py:404
  179.1 0.9 fusion.1
  180.0 0.0 copy-start
  180.0 12.1 %broadcast_select_fusion = (bf16[1,2,64,1,512,64]{4,5,3,2,1,0:T(8,128)(2,1)}, bf16[1,2,64,1,512,64]{4,5,3,2,1,0:T(8,128)(2,1)}) fusion(bf16[1,2,64,1,512,64]{4,5,3,2,1,0:T(8,128)(2,1)} %param.16, pred[2,64,512]{2,1,0:T(8,128)(4,1)S(1)} %iota_compare_fusion, bf16[2,64,64]{2,1,0:T(8,128)(2,1)S(1)} %get-tuple-element.9, ...), kind=kLoop, calls=%fused_computation | loop fusion | flops 8388608 | bytes 33652736 | tf_op jit(solution)/shard_map/jit(_where)/select_n | solution.py:420
  192.1 0.0 copy-done
  192.1 0.8 copy.17
  (1 shorter events, 0.0 us)
Async XLA Ops:
  180.0 12.1 %copy-start = (bf16[2,64,2048]{2,1,0:T(8,128)(2,1)S(1)}, bf16[2,64,2048]{2,1,0:T(8,128)(2,1)}, u32[]{:S(2)}) copy-start(bf16[2,64,2048]{2,1,0:T(8,128)(2,1)} %get-tuple-element.19) | copy-start | bytes 1572868
